TPU v7x, 256 devices: a 4x2x16 block of a 4x16x16 slice. The times are simulated.
256 devices in a mesh: groups: 2 (over y), gx: 32 (over z, core), gy: 4 (over x).
Axes of the slice: x: 4, y: 2, z: 16, core: 2. Of those that a mesh axis runs over, the one named last changes fastest.
The devices are a block of a 4x16x16 slice.
Arguments:
- hidden_in: bfloat16 [1024, 18432], P(('groups', 'gx'), 'gy'), parts along dimension 0, may hold values from -6 to 6
- w_query: bfloat16 [18432, 12288], P('gy', 'gx'), may hold values from -0.046875 to 0.046875
- w_out: bfloat16 [12288, 18432], P('gx', 'gy'), may hold values from -0.4375 to 0.4375
- cache_keys: bfloat16 [1024, 1024, 256], P(('groups', 'gx', 'gy')), parts along dimension 0, may hold values from -250 to 250
- cache_values: bfloat16 [1024, 1024, 256], P(('groups', 'gx', 'gy')), parts along dimension 0, may hold values from -6 to 6
- lengths: int32 [1024], P(('groups', 'gx', 'gy')), parts along dimension 0, may hold values from 128 to 1024
Outputs:
- layer_out: bfloat16 [1024, 18432], P(('groups', 'gx'), 'gy'), parts along dimension 0
There are 2 independent parts, one for each index of `groups`. A program takes and returns all parts, laid end to end along the dimension named above; an argument that names none is the same for every part. Nothing has to cross between parts.
All inputs are finite; a program needn't handle non-finite values.
Results may differ from a plain program's by a relative error of at most 0.0097.
Values may be sent and summed in bfloat16 or wider, within the bound.
A program may use at most 64 MiB of HBM per device.

v0:
```python
import jax
import jax.numpy as jnp
from jax import lax
from jax.sharding import Mesh
from jax.sharding import PartitionSpec as P

GX = ("gx_0", "gx_1")
GROUPS_GX = ("groups", "gx_0", "gx_1")
GROUPS_GX_GY = ("groups", "gx_0", "gx_1", "gy")


def cut_along(x, dim, size):
    dims = x.shape
    tiles = x.reshape(*dims[:dim], size, dims[dim] // size, *dims[dim + 1 :])
    return jnp.moveaxis(tiles, dim, 0)


def summed_on_arrival(x, axis, dim):
    size = lax.axis_size(axis)
    tiles = lax.all_to_all(cut_along(x, dim, size), axis, 0, 0, tiled=True)
    return jnp.sum(tiles, axis=0)


def reduced_to_own(tiles, axes, sequence):
    dims = [lax.axis_size(a) for a in axes]
    tiles = tiles.reshape(*dims, *tiles.shape[1:])
    tiles = tiles.transpose(*sequence, *range(len(axes), tiles.ndim))
    tiles = tiles.reshape(-1, *tiles.shape[len(axes) :])
    for k in sequence:
        tiles = lax.psum_scatter(tiles, axes[k], scatter_dimension=0, tiled=True)
    return tiles[0]


def sum_by_axis(x, axes, sequence, dim):
    size = lax.axis_size(axes)
    return reduced_to_own(cut_along(x, dim, size), axes, sequence)


def body(hidden_in, w_query, w_out, cache_keys, cache_values, lengths):
    across = lax.axis_size(GX)
    within = lax.axis_size("gy")
    local_seqs = cache_keys.shape[0]
    slot_count = cache_keys.shape[1]
    head_dim = cache_keys.shape[2]
    partial_query = jnp.dot(
        lax.all_gather(hidden_in, GX, axis=0, tiled=True),
        w_query,
        preferred_element_type=jnp.float32,
    )
    slice_width = partial_query.shape[1]
    grouped = partial_query.reshape(across, within, local_seqs, slice_width)
    own_rows = summed_on_arrival(grouped, "gy", 1)
    query_rows = own_rows.reshape(across * local_seqs, slice_width).astype(jnp.bfloat16)
    query = lax.all_to_all(query_rows, GX, split_axis=0, concat_axis=1, tiled=True)
    head_count = query.shape[1] // head_dim
    query_heads = query.reshape(local_seqs, head_count, head_dim)
    scores = jnp.einsum("bhd,bld->bhl", query_heads, cache_keys, preferred_element_type=jnp.float32)
    scores = scores / jnp.sqrt(jnp.float32(head_dim))
    live_slots = jnp.arange(slot_count)[None, None, :] < lengths[:, None, None]
    scores = jnp.where(live_slots, scores, jnp.float32(-1e30))
    top_score = jnp.max(scores, axis=2, keepdims=True)
    expo = jnp.where(live_slots, jnp.exp(scores - top_score), jnp.float32(0.0))
    probs = (expo / jnp.sum(expo, axis=2, keepdims=True)).astype(jnp.bfloat16)
    mixed = jnp.einsum("bhl,bld->bhd", probs, cache_values, preferred_element_type=jnp.float32)
    attended = mixed.astype(jnp.bfloat16).reshape(local_seqs, head_count * head_dim)
    spread = lax.all_to_all(attended, GX, split_axis=1, concat_axis=0, tiled=True)
    stacked = spread.reshape(across, local_seqs, slice_width)
    gathered = lax.all_gather(stacked, "gy", axis=1, tiled=True)
    head_rows = gathered.reshape(across * within * local_seqs, slice_width)
    result = sum_by_axis(
        jnp.dot(head_rows, w_out, preferred_element_type=jnp.float32), GX, (1, 0), 0
    )
    return result.astype(jnp.bfloat16)


def solution(mesh):
    torus = Mesh(
        mesh.devices.reshape(mesh.shape["groups"], 16, 2, mesh.shape["gy"]),
        ("groups", "gx_0", "gx_1", "gy"),
    )
    placed = (
        P(GROUPS_GX, "gy"),
        P("gy", GX),
        P(GX, "gy"),
        P(GROUPS_GX_GY, None, None),
        P(GROUPS_GX_GY, None, None),
        P(GROUPS_GX_GY),
    )
    return jax.shard_map(
        body, mesh=torus, in_specs=placed, out_specs=P(GROUPS_GX, "gy"), check_vma=False
    )
```

profile of v0, /device:TPU:36, one launch (start us, length us, event | category | flops | bytes accessed | tf_op | source)
XLA Modules:
  0.0 308.4 jit_solution(460804432666121327)
XLA Ops:
  6.5 0.0 copy-start
  6.6 0.0 all-gather.2.cloned.1.call-start
  6.6 0.7 all-gather.2.cloned.1.call-update
  7.3 87.8 %all-gather.2.cloned.1.call-done = bf16[512,4608]{1,0:T(8,128)(2,1)} async-done(((bf16[16,4608]{1,0:T(8,128)(2,1)}), bf16[512,4608]{1,0:T(8,128)(2,1)}) %all-gather.2.cloned.1.call-update) | async-done | bytes 4718608 | tf_op jit(solution)/shard_map/all_gather | solution.py:46
  95.1 6.9 %fusion.10 = f32[512,384]{1,0:T(8,128)} fusion(bf16[512,4608]{1,0:T(8,128)(2,1)} %all-gather.2.cloned.1.call-done, bf16[4608,384]{1,0:T(8,128)(2,1)} %param.7), kind=kOutput, calls=%fused_computation.17 | convolution fusion | flops 1811939328 | bytes 9043968 | tf_op jit(solution)/shard_map/dot_general | solution.py:45
  102.0 0.0 copy-start.2
  102.0 2.2 reshape_reshape.4
  104.2 1.2 copy.20
  105.5 14.7 %all_to_all.34 = f32[4,32,1,4,384]{4,3,1,2,0:T(4,128)} all-to-all(f32[4,32,1,4,384]{4,3,1,2,0:T(4,128)S(1)} %bitcast.25), channel_id=1, replica_groups=mesh['groups'=2,'gx_0'=16,'gx_1'=2,'gy'=4] {'gy'}, dimensions={0} | all-to-all | bytes 1572864 | tf_op jit(solution)/shard_map/all_to_all | solution.py:20
  120.1 2.0 reduce_sum.18
  122.1 8.8 %all-to-all-start.1 = ((bf16[32,4,384]{2,1,0:T(4,128)(2,1)}), bf16[32,4,384]{2,1,0:T(4,128)(2,1)}, u32[]{:S(2)}, u32[]{:S(2)}) async-start(bf16[32,4,384]{2,1,0:T(4,128)(2,1)} %reduce_sum.18), calls=%async_computation.1 | async-start | bytes 196608 | tf_op jit(solution)/shard_map/all_to_all | solution.py:54
  130.9 0.1 reduce-scatter.3.cloned.1.call-start
  131.0 0.0 copy-done.2
  131.0 0.1 iota_compare_fusion
  131.1 15.0 %all-to-all-done.1 = bf16[32,4,384]{2,1,0:T(4,128)(2,1)} async-done(((bf16[32,4,384]{2,1,0:T(4,128)(2,1)}), bf16[32,4,384]{2,1,0:T(4,128)(2,1)}, u32[]{:S(2)}, u32[]{:S(2)}) %all-to-all-start.1) | async-done | bytes 98336 | tf_op jit(solution)/shard_map/all_to_all | solution.py:54
  146.1 1.5 copy.12
  147.6 1.6 reshape.48
  149.2 2.4 fusion.5
  151.6 0.0 copy-start.1
  151.6 0.9 copy-done.1
  152.5 0.3 fusion.9
  152.8 3.2 %convolution_convert_fusion = bf16[4,48,256]{2,1,0:T(8,128)(2,1)} fusion(bf16[4,1024,256]{2,1,0:T(8,128)(2,1)} %param.10, f32[4,48]{1,0:T(4,128)S(1)} %fusion.9, f32[4,48,1024]{2,1,0:T(8,128)} %copy-done.1, pred[4,1024]{1,0:T(4,128)(4,1)S(1)} %iota_compare_fusion), kind=kOutput, calls=%fused_computation.8 | convolution fusion | flops 101500096 | bytes 2986752 | tf_op jit(solution)/shard_map/bhl,bld->bhd/dot_general | solution.py:64
  156.0 1.6 all_to_all.28
  157.6 0.9 copy.13
  158.6 18.9 %all_to_all.35 = bf16[4,32,384]{2,0,1:T(4,128)(2,1)S(1)} all-to-all(bf16[4,32,384]{2,0,1:T(4,128)(2,1)S(1)} %copy.13), channel_id=1, replica_groups=mesh['groups'=2,'gx_0'=16,'gx_1'=2,'gy'=4] {'gx_0','gx_1'}, dimensions={1} | all-to-all | bytes 196608 | tf_op jit(solution)/shard_map/all_to_all | solution.py:66
  177.5 13.6 %all_gather.7 = bf16[32,16,384]{2,0,1:T(8,128)(2,1)S(1)} all-gather(bf16[32,4,384]{2,0,1:T(8,128)(2,1)S(1)} %copy.14), channel_id=1, replica_groups=mesh['groups'=2,'gx_0'=16,'gx_1'=2,'gy'=4] {'gy'}, dimensions={1}, use_global_device_ids=true | all-gather | bytes 491520 | tf_op jit(solution)/shard_map/all_gather | solution.py:68
  191.1 0.1 copy.15
  191.2 0.0 copy-done
  191.2 2.6 convolution_bitcast_fusion
  193.8 4.2 %copy.16 = f32[2,16,16,4608]{3,2,1,0:T(8,128)} copy(f32[2,16,16,4608]{3,2,0,1:T(8,128)S(1)} %convolution_bitcast_fusion) | data formatting | bytes 18874368 | tf_op jit(solution)/shard_map/transpose | solution.py:27
  198.1 0.1 reduce-scatter.3.cloned.1.call-update
  198.2 0.1 reduce-scatter.5.cloned.1.call-start
  198.2 17.6 %reduce-scatter.3.cloned.1.call-done = f32[16,16,4608]{2,1,0:T(8,128)} async-done(((f32[32,16,4608]{2,1,0:T(8,128)}), f32[16,16,4608]{2,1,0:T(8,128)}) %reduce-scatter.3.cloned.1.call-update) | async-done | bytes 4718608 | tf_op jit(solution)/shard_map/reduce_scatter | solution.py:30
  215.8 0.1 reduce-scatter.5.cloned.1.call-update
  215.9 84.3 %reduce-scatter.5.cloned.1.call-done = f32[1,16,4608]{2,1,0:T(8,128)} async-done(((f32[16,16,4608]{2,1,0:T(8,128)}), f32[1,16,4608]{2,1,0:T(8,128)}) %reduce-scatter.5.cloned.1.call-update) | async-done | bytes 294928 | tf_op jit(solution)/shard_map/reduce_scatter | solution.py:30
  300.2 1.6 convert_bitcast_fusion
  (1 shorter events, 0.0 us)
Async XLA Ops:
  6.5 184.7 %copy-start = (bf16[384,4608]{1,0:T(8,128)(2,1)S(1)}, bf16[384,4608]{1,0:T(8,128)(2,1)}, u32[]{:S(2)}) copy-start(bf16[384,4608]{1,0:T(8,128)(2,1)} %param.8) | copy-start | bytes 10616836
  6.6 88.5 %all-gather.2.cloned.1.call-start = ((), (), s32[]{:S(2)}) async-start(), calls=%async_computation.5 | async-start | bytes 4866048 | tf_op jit(solution)/shard_map/all_gather | solution.py:46
  102.0 29.0 %copy-start.2 = (s32[4]{0:T(128)S(1)}, s32[4]{0:T(128)}, u32[]{:S(2)}) copy-start(s32[4]{0:T(128)} %param.11) | copy-start | bytes 52
  122.1 24.0 %all-to-all-start.1 = ((bf16[32,4,384]{2,1,0:T(4,128)(2,1)}), bf16[32,4,384]{2,1,0:T(4,128)(2,1)}, u32[]{:S(2)}, u32[]{:S(2)}) async-start(bf16[32,4,384]{2,1,0:T(4,128)(2,1)} %reduce_sum.18), calls=%async_computation.1 | async-start | bytes 196608 | tf_op jit(solution)/shard_map/all_to_all | solution.py:54
  130.9 84.9 %reduce-scatter.3.cloned.1.call-start = ((), (), s32[]{:S(2)}) async-start(), calls=%async_computation.6 | async-start | bytes 14155776 | tf_op jit(solution)/shard_map/reduce_scatter | solution.py:30
  151.6 0.9 copy-start.1
  198.2 102.1 %reduce-scatter.5.cloned.1.call-start = ((), (), s32[]{:S(2)}) async-start(), calls=%async_computation.7 | async-start | bytes 5013504 | tf_op jit(solution)/shard_map/reduce_scatter | solution.py:30
Sparse Core Ops, SparseCore 0:
  9.2 85.8 all-gather.1
  198.3 17.4 reduce-scatter.2
  218.4 81.7 reduce-scatter.4
where the time goes:
time: 309 us; the launch traced here: 308 us
  waiting for transfers between devices  206 us (67%)
  blocking collectives  47.2 us (15%)
  matrix products  15.2 us (5%)
  local copies, waits for them, and re-layouts  14.4 us (5%)
  between operations  13.2 us (4%)
  starting transfers between devices  8.93 us (3%)
  other arithmetic  3.99 us (1%)
    reduce_scatter x2, waiting for transfers between devices, reduced_to_own(): tiles = lax.psum_scatter(tiles, axes[k], scatter_dimension=0, tiled=True)  102 us
    all_gather x1, waiting for transfers between devices, body(): lax.all_gather(hidden_in, GX, axis=0, tiled=True)  87.8 us
    all_to_all x1, blocking collectives, body(): lax.all_to_all(attended, GX, split_axis=1, concat_axis=0, tiled=True)  18.9 us
    all_to_all x1, waiting for transfers between devices, body(): lax.all_to_all(query_rows, GX, split_axis=0, concat_axis=1, tiled=True)  15 us
    all_to_all x1, blocking collectives, summed_on_arrival(): tiles = lax.all_to_all(cut_along(x, dim, size), axis, 0, 0, tiled=True)  14.7 us
    all_gather x1, blocking collectives, body(): gathered = lax.all_gather(stacked, 'gy', axis=1, tiled=True)  13.6 us
    all_to_all x1, starting transfers between devices, body(): lax.all_to_all(query_rows, GX, split_axis=0, concat_axis=1, tiled=True)  8.8 us
    dot_general x1, matrix products, body(): jnp.dot(lax.all_gather(hidden_in, GX, axis=0, tiled=True), w_query, prefe...  6.93 us
  transfers between devices with their start and end apart: 4, of which 4 were waited for; matrix products, arithmetic and copies ran while one was open for 0% of the time, Pallas kernels for 0%

commit v1 on v0

--- a/solution.py
+++ b/solution.py
@@ -1,12 +1,30 @@
+import functools
 import jax
 import jax.numpy as jnp
 from jax import lax
 from jax.sharding import Mesh
 from jax.sharding import PartitionSpec as P
+from jax.lax import all_to_all, axis_size
 
 GX = ("gx_0", "gx_1")
 GROUPS_GX = ("groups", "gx_0", "gx_1")
 GROUPS_GX_GY = ("groups", "gx_0", "gx_1", "gy")
+
+
+def advance_skins_for(array_in, mesh_ax):
+    built = jnp.concatenate(
+        all_to_all(
+            jnp.stack(tuple((array_in for _ in range(axis_size(mesh_ax)))), 0),
+            axis_name=mesh_ax,
+            split_axis=0,
+            concat_axis=0,
+        ),
+        0,
+    )
+    return built
+
+
+_draw_rates = functools.partial(advance_skins_for, mesh_ax=GX)
 
 
 def cut_along(x, dim, size):
@@ -42,11 +60,7 @@
     local_seqs = cache_keys.shape[0]
     slot_count = cache_keys.shape[1]
     head_dim = cache_keys.shape[2]
-    partial_query = jnp.dot(
-        lax.all_gather(hidden_in, GX, axis=0, tiled=True),
-        w_query,
-        preferred_element_type=jnp.float32,
-    )
+    partial_query = jnp.dot(_draw_rates(hidden_in), w_query, preferred_element_type=jnp.float32)
     slice_width = partial_query.shape[1]
     grouped = partial_query.reshape(across, within, local_seqs, slice_width)
     own_rows = summed_on_arrival(grouped, "gy", 1)

time: 309 us -> 453 us (1.47)
  blocking collectives: 47.2 us -> 285 us
  waiting for transfers between devices: 206 us -> 117 us
    all_to_all x0 -> x1, blocking collectives: none -> 237 us  [advance_skins_for(): all_to_all(jnp.stack(tuple((array_in for _ in range(axis_size(mesh_ax))))...]
    all_gather x1 -> x0, waiting for transfers between devices: 87.8 us -> none  [body(): lax.all_gather(hidden_in, GX, axis=0, tiled=True)]
  transfers between devices with their start and end apart: 4 -> 3, of which waited for: 4 -> 3; matrix products, arithmetic and copies ran while one was open for 0% -> 0% of each run, Pallas kernels for 0% -> 0%
where the time goes in v1:
time: 453 us; the launch traced here: 452 us
  blocking collectives  285 us (63%)
  waiting for transfers between devices  117 us (26%)
  local copies, waits for them, and re-layouts  16.7 us (4%)
  between operations  13.5 us (3%)
  matrix products  10.8 us (2%)
  starting transfers between devices  5.51 us (1%)
    all_to_all x1, blocking collectives, advance_skins_for(): all_to_all(jnp.stack(tuple((array_in for _ in range(axis_size(mesh_ax))))...  237 us
    reduce_scatter x2, waiting for transfers between devices, reduced_to_own(): tiles = lax.psum_scatter(tiles, axes[k], scatter_dimension=0, tiled=True)  102 us
    all_to_all x1, blocking collectives, body(): lax.all_to_all(attended, GX, split_axis=1, concat_axis=0, tiled=True)  18.9 us
    all_to_all x1, waiting for transfers between devices, body(): lax.all_to_all(query_rows, GX, split_axis=0, concat_axis=1, tiled=True)  14.9 us
    all_to_all x1, blocking collectives, summed_on_arrival(): tiles = lax.all_to_all(cut_along(x, dim, size), axis, 0, 0, tiled=True)  14.5 us
    all_gather x1, blocking collectives, body(): gathered = lax.all_gather(stacked, 'gy', axis=1, tiled=True)  13.8 us
  transfers between devices with their start and end apart: 3, of which 3 were waited for; matrix products, arithmetic and copies ran while one was open for 0% of the time, Pallas kernels for 0%

profile of v1, /device:TPU:36, one launch (start us, length us, event | category | flops | bytes accessed | tf_op | source)
XLA Modules:
  0.0 452.4 jit_solution(3791627587275040087)
XLA Ops:
  6.5 0.0 copy-start
  6.6 1.6 stack.2
  8.1 237.5 %all_to_all.39 = bf16[32,16,4608]{2,1,0:T(8,128)(2,1)S(1)} all-to-all(bf16[32,16,4608]{2,1,0:T(8,128)(2,1)S(1)} %stack.2), channel_id=1, replica_groups=mesh['groups'=2,'gx_0'=16,'gx_1'=2,'gy'=4] {'gx_0','gx_1'}, dimensions={0} | all-to-all | bytes 9437184 | tf_op jit(solution)/shard_map/all_to_all | solution.py:16
  245.6 0.0 copy-start.3
  245.6 2.6 copy.17
  248.2 0.0 copy-done.3
  248.2 0.0 copy-start.2
  248.2 2.6 fusion.5
  250.8 14.5 %all_to_all.40 = f32[4,32,1,4,384]{4,1,3,2,0:T(8,128)} all-to-all(f32[4,32,1,4,384]{4,1,3,2,0:T(8,128)S(1)} %fusion.5), channel_id=1, replica_groups=mesh['groups'=2,'gx_0'=16,'gx_1'=2,'gy'=4] {'gy'}, dimensions={0} | all-to-all | bytes 1572864 | tf_op jit(solution)/shard_map/all_to_all | solution.py:38
  265.3 1.8 reduce_sum.18
  267.1 1.6 copy.19
  268.7 5.4 %all-to-all-start.2 = ((bf16[32,4,384]{2,1,0:T(4,128)(2,1)}), bf16[32,4,384]{2,1,0:T(4,128)(2,1)}, u32[]{:S(2)}, u32[]{:S(2)}) async-start(bf16[32,4,384]{2,1,0:T(4,128)(2,1)} %copy.19), calls=%async_computation.2 | async-start | bytes 196608 | tf_op jit(solution)/shard_map/all_to_all | solution.py:68
  274.1 0.1 reduce-scatter.3.cloned.1.call-start
  274.2 0.0 copy-done.2
  274.2 0.1 iota_compare_fusion
  274.3 14.9 %all-to-all-done.2 = bf16[32,4,384]{2,1,0:T(4,128)(2,1)} async-done(((bf16[32,4,384]{2,1,0:T(4,128)(2,1)}), bf16[32,4,384]{2,1,0:T(4,128)(2,1)}, u32[]{:S(2)}, u32[]{:S(2)}) %all-to-all-start.2) | async-done | bytes 98336 | tf_op jit(solution)/shard_map/all_to_all | solution.py:68
  289.2 1.5 copy.20
  290.7 1.6 reshape.59
  292.3 2.4 fusion.10
  294.7 0.0 copy-start.1
  294.7 0.9 copy-done.1
  295.6 0.3 fusion.14
  295.9 3.2 convolution_convert_fusion
  299.1 1.6 all_to_all.32
  300.7 0.9 copy.21
  301.7 18.9 %all_to_all.41 = bf16[4,32,384]{2,0,1:T(4,128)(2,1)S(1)} all-to-all(bf16[4,32,384]{2,0,1:T(4,128)(2,1)S(1)} %copy.21), channel_id=1, replica_groups=mesh['groups'=2,'gx_0'=16,'gx_1'=2,'gy'=4] {'gx_0','gx_1'}, dimensions={1} | all-to-all | bytes 196608 | tf_op jit(solution)/shard_map/all_to_all | solution.py:80
  320.5 13.8 %all_gather.3 = bf16[32,16,384]{2,0,1:T(8,128)(2,1)S(1)} all-gather(bf16[32,4,384]{2,0,1:T(8,128)(2,1)S(1)} %copy.22), channel_id=1, replica_groups=mesh['groups'=2,'gx_0'=16,'gx_1'=2,'gy'=4] {'gy'}, dimensions={1}, use_global_device_ids=true | all-gather | bytes 491520 | tf_op jit(solution)/shard_map/all_gather | solution.py:82
  334.3 0.1 copy.23
  334.5 0.0 copy-done
  334.5 2.6 convolution_bitcast_fusion
  337.1 4.2 copy.24
  341.3 0.1 reduce-scatter.3.cloned.1.call-update
  341.4 0.1 reduce-scatter.5.cloned.1.call-start
  341.5 18.2 %reduce-scatter.3.cloned.1.call-done = f32[16,16,4608]{2,1,0:T(8,128)} async-done(((f32[32,16,4608]{2,1,0:T(8,128)}), f32[16,16,4608]{2,1,0:T(8,128)}) %reduce-scatter.3.cloned.1.call-update) | async-done | bytes 4718608 | tf_op jit(solution)/shard_map/reduce_scatter | solution.py:48
  359.7 0.1 reduce-scatter.5.cloned.1.call-update
  359.7 84.1 %reduce-scatter.5.cloned.1.call-done = f32[1,16,4608]{2,1,0:T(8,128)} async-done(((f32[16,16,4608]{2,1,0:T(8,128)}), f32[1,16,4608]{2,1,0:T(8,128)}) %reduce-scatter.5.cloned.1.call-update) | async-done | bytes 294928 | tf_op jit(solution)/shard_map/reduce_scatter | solution.py:48
  443.9 1.6 convert_bitcast_fusion
  (1 shorter events, 0.0 us)
Async XLA Ops:
  6.5 327.9 %copy-start = (bf16[384,4608]{1,0:T(8,128)(2,1)S(1)}, bf16[384,4608]{1,0:T(8,128)(2,1)}, u32[]{:S(2)}) copy-start(bf16[384,4608]{1,0:T(8,128)(2,1)} %param.8) | copy-start | bytes 10616836
  245.6 2.6 copy-start.3
  248.2 25.9 %copy-start.2 = (s32[4]{0:T(128)S(1)}, s32[4]{0:T(128)}, u32[]{:S(2)}) copy-start(s32[4]{0:T(128)} %param.11) | copy-start | bytes 52
  268.7 20.5 %all-to-all-start.2 = ((bf16[32,4,384]{2,1,0:T(4,128)(2,1)}), bf16[32,4,384]{2,1,0:T(4,128)(2,1)}, u32[]{:S(2)}, u32[]{:S(2)}) async-start(bf16[32,4,384]{2,1,0:T(4,128)(2,1)} %copy.19), calls=%async_computation.2 | async-start | bytes 196608 | tf_op jit(solution)/shard_map/all_to_all | solution.py:68
  274.1 85.6 %reduce-scatter.3.cloned.1.call-start = ((), (), s32[]{:S(2)}) async-start(), calls=%async_computation.6 | async-start | bytes 14155776 | tf_op jit(solution)/shard_map/reduce_scatter | solution.py:48
  294.7 0.9 copy-start.1
  341.4 102.5 %reduce-scatter.5.cloned.1.call-start = ((), (), s32[]{:S(2)}) async-start(), calls=%async_computation.7 | async-start | bytes 5013504 | tf_op jit(solution)/shard_map/reduce_scatter | solution.py:48
Sparse Core Ops, SparseCore 0:
  341.5 18.1 reduce-scatter.2
  362.3 81.5 reduce-scatter.4
